TPU v7x, 32 devices: a whole 2x2x4 slice. The times are simulated.
32 devices in a mesh: req: 8 (over z, core), blk: 4 (over y, x).
Axes of the slice: x: 2, y: 2, z: 4, core: 2. Of those that a mesh axis runs over, the one named last changes fastest.
Arguments:
- draft_node_queries: bfloat16 [256, 4096], P(('req', 'blk')), parts along dimension 0, may hold values from -6 to 6, as said below
- draft_node_keys: bfloat16 [256, 512], P(('req', 'blk')), parts along dimension 0, may hold values from -6 to 6
- draft_node_values: bfloat16 [256, 512], P(('req', 'blk')), parts along dimension 0, may hold values from -6 to 6
- paged_key_cache: bfloat16 [16384, 512], P(('req', 'blk')), parts along dimension 0, may hold values from -6 to 6
- paged_value_cache: bfloat16 [16384, 512], P(('req', 'blk')), parts along dimension 0, may hold values from -6 to 6
- context_length: int32 [8], P('req'), parts along dimension 0, may hold values from 1024 to 2048
- parents: int32 [256], P('req'), parts along dimension 0, may hold values from 0 to 31, as said below
- accepted_path: int32 [64], P('req'), parts along dimension 0, may hold values from 0 to 31, as said below
- out_weight: bfloat16 [2880, 4096], P('blk'), may hold values from -0.09375 to 0.09375
Outputs:
- tree_attention: bfloat16 [256, 4096], P(('req', 'blk')), parts along dimension 0
- path_output: bfloat16 [64, 2880], P('req', 'blk'), parts along dimension 0
There are 8 independent parts, one for each index of `req`. A program takes and returns all parts, laid end to end along the dimension named above; an argument that names none is the same for every part. Nothing has to cross between parts.
Inputs may be any that keep to these rules, and one draw needn't show every extreme that they name: `draft_node_queries`: query entries lie within the range. parents[0] = 0 marks the root; for i >= 1, parents[i] is one of the nodes i - 4 to i - 1 (and at least 0). `accepted_path`: distinct nodes; each entry after the first is a child of the one before it.
All inputs are finite; a program needn't handle non-finite values.
Results may differ from a plain program's by a relative error of at most 0.0095.
Values may be sent and summed in bfloat16 or wider, within the bound.
A program may use at most 64 MiB of HBM per device.

v0:
```python
import functools
import math

import jax
import jax.numpy as jnp
from jax import lax
from jax.experimental import pallas as pl
from jax.experimental.pallas import tpu as pltpu
from jax.sharding import PartitionSpec as P

QUERY_HEADS = 64
KEY_VALUE_HEADS = 8
HEAD_WIDTH = 64
GROUP = QUERY_HEADS // KEY_VALUE_HEADS
LANES = 128
CHUNKS = KEY_VALUE_HEADS * HEAD_WIDTH // LANES
CHUNK = 2 * GROUP * HEAD_WIDTH
PAIRS = CHUNK // LANES
HEADS = 2 * GROUP
EXCLUDED = -1e30
FLOOR = -1e20
SCALE = HEAD_WIDTH ** (-0.5)
NT = (((1,), (1,)), ((), ()))
MESH = pl.DeviceIdType.MESH


def partner(me, k, n):
    if n & (n - 1):
        return lax.rem(me + k, n)
    other = me
    bit = 1
    while bit < n:
        if k & bit:
            other = other + bit - 2 * bit * ((me // bit) % 2)
        bit *= 2
    return other


def kernel(
    n, own, nodes,
    length_hbm, parents_hbm, path_hbm, q_ref, k_ref, v_ref, kc_ref, vc_ref, w_ref,
    att_ref, out_ref,
    length_ref, parents_ref, path_ref, kown, vown,
    qbuf, kbuf, vbuf, wbuf, bias, sbuf, rbuf, acc,
    load_sem, q_load_sem, q_send, q_recv, p_send, p_recv,
):
    me = lax.axis_index("blk")
    rows = q_ref.shape[0]
    wide = n * rows
    cached = kc_ref.shape[0]
    picked = path_hbm.shape[0]
    peers = [partner(me, k, n) for k in range(n - 1, 0, -1)]

    q_loads = [
        pltpu.make_async_copy(
            q_ref.at[:, pl.ds(c * CHUNK, CHUNK)], qbuf.at[c, me], q_load_sem.at[c]
        )
        for c in range(CHUNKS)
    ]
    for copy in q_loads:
        copy.start()
    load_k = pltpu.make_async_copy(kc_ref, kbuf.at[pl.ds(0, cached)], load_sem.at[0])
    load_v = pltpu.make_async_copy(vc_ref, vbuf.at[pl.ds(0, cached)], load_sem.at[1])
    load_w = pltpu.make_async_copy(w_ref, wbuf, load_sem.at[2])

    small_loads = [
        pltpu.make_async_copy(src, dst, load_sem.at[3 + i])
        for i, (src, dst) in enumerate((
            (parents_hbm, parents_ref), (length_hbm, length_ref), (path_hbm, path_ref),
            (k_ref, kown), (v_ref, vown),
        ))
    ]
    for copy in small_loads:
        copy.start()

    barrier = pltpu.get_barrier_semaphore()
    for peer in peers:
        pl.semaphore_signal(barrier, inc=1, device_id={"blk": peer}, device_id_type=MESH)
    pl.semaphore_wait(barrier, n - 1)

    def q_copy(c, slot, peer):
        return pltpu.make_async_remote_copy(
            src_ref=qbuf.at[c, slot], dst_ref=qbuf.at[c, slot],
            send_sem=q_send.at[c, peer], recv_sem=q_recv.at[c, slot],
            device_id={"blk": peer}, device_id_type=MESH,
        )

    def p_copy(c, slot, peer):
        return pltpu.make_async_remote_copy(
            src_ref=sbuf.at[c, peer], dst_ref=rbuf.at[c, slot],
            send_sem=p_send.at[c, peer], recv_sem=p_recv.at[c, slot],
            device_id={"blk": peer}, device_id_type=MESH,
        )

    for c in range(CHUNKS):
        q_loads[c].wait()
        for peer in peers:
            q_copy(c, me, peer).start()
    load_k.start()
    load_v.start()
    load_w.start()

    for copy in small_loads:
        copy.wait()
    blank = jnp.zeros((LANES - rows, k_ref.shape[1]), jnp.float32)
    for ref, buf in ((kown, kbuf), (vown, vbuf)):
        buf[pl.ds(cached, LANES)] = jnp.concatenate(
            [ref[...].astype(jnp.float32), blank], axis=0
        ).astype(jnp.bfloat16)

    up = lax.broadcasted_iota(jnp.int32, (wide, wide), 0)
    down = lax.broadcasted_iota(jnp.int32, (wide, wide), 1)
    up_node = up // rows * own + up % rows
    links = jnp.where(up == down, 1.0, 0.0)
    for i in range(1, nodes):
        at = i // own * rows + i % own
        links = jnp.where((down == at) & (up_node == parents_ref[i]) & (up % rows < own), 1.0, links)
    for squaring in range(max(1, math.ceil(math.log2(nodes)))):
        half = links.astype(jnp.bfloat16)
        links = jnp.minimum(jnp.dot(half, half, preferred_element_type=jnp.float32), 1.0)
    source = lax.broadcasted_iota(jnp.int32, (wide, LANES), 0)
    column = lax.broadcasted_iota(jnp.int32, (wide, LANES), 1)
    mine = jnp.where((source == me * rows + column) & (column < own), 1.0, 0.0)
    related = lax.dot_general(
        links.astype(jnp.bfloat16), mine.astype(jnp.bfloat16), (((0,), (0,)), ((), ())),
        preferred_element_type=jnp.float32,
    )
    position = lax.broadcasted_iota(jnp.int32, (wide, cached), 1) + me * cached
    bias[:, pl.ds(0, cached)] = jnp.where(position < length_ref[0], 0.0, EXCLUDED)
    bias[:, pl.ds(cached, LANES)] = jnp.where(related > 0.5, 0.0, EXCLUDED)

    which = lax.broadcasted_iota(jnp.int32, (picked, wide), 0)
    spot = lax.broadcasted_iota(jnp.int32, (picked, wide), 1)
    spot_node = spot // rows * own + spot % rows
    wanted = jnp.full((picked, wide), -1, jnp.int32)
    for k in range(picked):
        wanted = jnp.where(which == k, path_ref[k], wanted)
    picker = jnp.where((wanted == spot_node) & (spot % rows < own), 1.0, 0.0)
    picker_half = picker.astype(jnp.bfloat16)

    load_k.wait()
    load_v.wait()
    lane = lax.broadcasted_iota(jnp.int32, (wide, LANES), 1)
    low = lane < HEAD_WIDTH

    def attend(c, unused):
        for peer in peers:
            q_copy(c, peer, peer).wait_recv()
        q = qbuf[c].astype(jnp.float32).reshape(wide, CHUNK)
        columns = pl.ds(pl.multiple_of(c * LANES, LANES), LANES)
        keys = kbuf[:, columns]
        values = vbuf[:, columns]
        tiles = []
        logs = jnp.full((wide, LANES), EXCLUDED, jnp.float32)
        for side in range(2):
            keep = low if side == 0 else jnp.logical_not(low)
            stacked = []
            for pair in range(PAIRS // 2):
                start = (side * PAIRS // 2 + pair) * LANES
                tile = q[:, start : start + LANES]
                turned = pltpu.roll(tile, HEAD_WIDTH, 1)
                even, odd = (tile, turned) if side == 0 else (turned, tile)
                stacked.append(jnp.where(keep, even, 0.0))
                stacked.append(jnp.where(keep, odd, 0.0))
            queries = jnp.concatenate(stacked, axis=0).astype(jnp.bfloat16)
            scores = lax.dot_general(queries, keys, NT, preferred_element_type=jnp.float32)
            scores = (
                scores.reshape(GROUP, wide, cached + LANES) + bias[...][None]
            ).reshape(GROUP * wide, cached + LANES)
            top = jnp.maximum(jnp.max(scores, axis=-1, keepdims=True), FLOOR)
            weights = jnp.exp2((scores - top) * (SCALE * math.log2(math.e)))
            total = jnp.sum(weights, axis=-1, keepdims=True)
            weighted = jnp.dot(
                weights.astype(jnp.bfloat16), values, preferred_element_type=jnp.float32
            )
            some = total > 0.0
            safe = jnp.where(some, total, 1.0)
            weighted = weighted / safe
            level = jnp.where(some, top * SCALE + jnp.log(safe), EXCLUDED)
            for head in range(GROUP):
                logs = jnp.where(
                    lane == side * GROUP + head, level[head * wide : (head + 1) * wide], logs
                )
            for pair in range(PAIRS // 2):
                even = weighted[2 * pair * wide : (2 * pair + 1) * wide]
                odd = weighted[(2 * pair + 1) * wide : (2 * pair + 2) * wide]
                if side == 0:
                    odd = pltpu.roll(odd, HEAD_WIDTH, 1)
                else:
                    even = pltpu.roll(even, HEAD_WIDTH, 1)
                tiles.append(jnp.where(low, even, odd))
        first = logs.astype(jnp.bfloat16).astype(jnp.float32)
        rest = logs - first
        second = rest.astype(jnp.bfloat16).astype(jnp.float32)
        third = rest - second
        tiles.append(
            jnp.where(
                lane < HEADS, first,
                jnp.where(
                    lane < 2 * HEADS, pltpu.roll(second, HEADS, 1),
                    jnp.where(lane < 3 * HEADS, pltpu.roll(third, 2 * HEADS, 1), 0.0),
                ),
            )
        )
        part = jnp.concatenate(tiles, axis=1)
        path_part = jnp.dot(
            picker_half, part.astype(jnp.bfloat16), preferred_element_type=jnp.float32
        )
        for d in range(n):
            mine = slice(d * rows, (d + 1) * rows)
            sbuf[c, d] = jnp.concatenate([part[mine], path_part], axis=0).astype(jnp.bfloat16)
        for peer in peers:
            p_copy(c, me, peer).start()
        return unused

    lax.fori_loop(0, CHUNKS, attend, 0, unroll=True)
    load_w.wait()
    acc[...] = jnp.zeros_like(acc)
    low_out = lax.broadcasted_iota(jnp.int32, (rows + picked, LANES), 1) < HEAD_WIDTH

    def finish(c, unused):
        for peer in peers:
            p_copy(c, peer, peer).wait_recv()
        parts = [sbuf[c, me]] + [rbuf[c, peer] for peer in peers]
        logs = []
        for part in parts:
            terms = part[:, CHUNK:].astype(jnp.float32)
            logs.append(
                terms
                + pltpu.roll(terms, LANES - HEADS, 1)
                + pltpu.roll(terms, LANES - 2 * HEADS, 1)
            )
        top = functools.reduce(jnp.maximum, logs)
        shares = [jnp.exp(log - top) for log in logs]
        total = functools.reduce(jnp.add, shares)
        shares = [share / total for share in shares]
        tiles = []
        for pair in range(PAIRS):
            span = slice(pair * LANES, (pair + 1) * LANES)
            tile = jnp.zeros((rows + picked, LANES), jnp.float32)
            for share, part in zip(shares, parts):
                factor = jnp.where(
                    low_out, share[:, 2 * pair : 2 * pair + 1], share[:, 2 * pair + 1 : 2 * pair + 2]
                )
                tile = tile + factor * part[:, span].astype(jnp.float32)
            tiles.append(tile)
        rows_done = jnp.concatenate(tiles, axis=1)
        columns = pl.ds(pl.multiple_of(c * CHUNK, CHUNK), CHUNK)
        att_ref[:, columns] = rows_done[:rows].astype(jnp.bfloat16)
        acc[...] += lax.dot_general(
            rows_done[rows:].astype(jnp.bfloat16), wbuf[:, columns], NT,
            preferred_element_type=jnp.float32,
        )
        return unused

    lax.fori_loop(0, CHUNKS, finish, 0, unroll=True)
    out_ref[...] = acc[...].astype(jnp.bfloat16)

    def drain(c, unused):
        for peer in peers:
            q_copy(c, me, peer).wait_send()
            p_copy(c, me, peer).wait_send()
        return unused

    lax.fori_loop(0, CHUNKS, drain, 0)


def write_out(att_ref, out_ref, att_hbm, out_hbm, sems):
    copies = [
        pltpu.make_async_copy(att_ref, att_hbm, sems.at[0]),
        pltpu.make_async_copy(out_ref, out_hbm, sems.at[1]),
    ]
    for copy in copies:
        copy.start()
    for copy in copies:
        copy.wait()


def local(
    n,
    draft_node_queries,
    draft_node_keys,
    draft_node_values,
    paged_key_cache,
    paged_value_cache,
    context_length,
    parents,
    accepted_path,
    out_weight,
):
    own = draft_node_queries.shape[0]
    rows = -(-own // 8) * 8
    if rows != own:
        pad = ((0, rows - own), (0, 0))
        draft_node_queries = jnp.pad(draft_node_queries, pad)
        draft_node_keys = jnp.pad(draft_node_keys, pad)
        draft_node_values = jnp.pad(draft_node_values, pad)
    wide = n * rows
    cached, cache_width = paged_key_cache.shape
    picked = accepted_path.shape[0]
    vmem = pl.BlockSpec(memory_space=pltpu.VMEM)
    anywhere = pl.BlockSpec(memory_space=pltpu.HBM)
    shapes = (
        jax.ShapeDtypeStruct((rows, QUERY_HEADS * HEAD_WIDTH), jnp.bfloat16),
        jax.ShapeDtypeStruct((picked, out_weight.shape[0]), jnp.bfloat16),
    )
    held = pl.pallas_call(
        functools.partial(kernel, n, own, parents.shape[0]),
        out_shape=tuple(pltpu.VMEM(shape.shape, shape.dtype) for shape in shapes),
        in_specs=[anywhere] * 9,
        out_specs=(vmem, vmem),
        scratch_shapes=[
            pltpu.SMEM(context_length.shape, jnp.int32),
            pltpu.SMEM(parents.shape, jnp.int32),
            pltpu.SMEM(accepted_path.shape, jnp.int32),
            pltpu.VMEM((rows, cache_width), jnp.bfloat16),
            pltpu.VMEM((rows, cache_width), jnp.bfloat16),
            pltpu.VMEM((CHUNKS, n, rows, CHUNK), jnp.bfloat16),
            pltpu.VMEM((cached + LANES, cache_width), jnp.bfloat16),
            pltpu.VMEM((cached + LANES, cache_width), jnp.bfloat16),
            pltpu.VMEM(out_weight.shape, jnp.bfloat16),
            pltpu.VMEM((wide, cached + LANES), jnp.float32),
            pltpu.VMEM((CHUNKS, n, rows + picked, CHUNK + LANES), jnp.bfloat16),
            pltpu.VMEM((CHUNKS, n, rows + picked, CHUNK + LANES), jnp.bfloat16),
            pltpu.VMEM((picked, out_weight.shape[0]), jnp.float32),
            pltpu.SemaphoreType.DMA((8,)),
            pltpu.SemaphoreType.DMA((CHUNKS,)),
        ]
        + [pltpu.SemaphoreType.DMA((CHUNKS, n))] * 4,
        compiler_params=pltpu.CompilerParams(
            collective_id=0, has_side_effects=True, vmem_limit_bytes=56 * 1024 * 1024
        ),
        name="verify_tree",
    )(
        context_length, parents, accepted_path,
        draft_node_queries, draft_node_keys, draft_node_values,
        paged_key_cache, paged_value_cache, out_weight,
    )
    attention, path_output = pl.pallas_call(
        write_out,
        out_shape=shapes,
        in_specs=(vmem, vmem),
        out_specs=(anywhere, anywhere),
        scratch_shapes=[pltpu.SemaphoreType.DMA((2,))],
        compiler_params=pltpu.CompilerParams(vmem_limit_bytes=1024 * 1024),
        name="write_out",
    )(*held)
    return attention[:own], path_output


def solution(mesh):
    in_specs = (
        P(("req", "blk"), None),
        P(("req", "blk"), None),
        P(("req", "blk"), None),
        P(("req", "blk"), None),
        P(("req", "blk"), None),
        P("req"),
        P("req"),
        P("req"),
        P("blk", None),
    )
    out_specs = (P(("req", "blk"), None), P("req", "blk"))
    return jax.shard_map(
        functools.partial(local, mesh.shape["blk"]),
        mesh=mesh, in_specs=in_specs, out_specs=out_specs, check_vma=False,
    )
```

profile of v0, /device:TPU:0, one launch (start us, length us, event | category | flops | bytes accessed | tf_op | source)
XLA Modules:
  0.0 19.2 jit_solution(11434262040569546139)
XLA Ops:
  1.3 17.3 %verify_tree.1 = (bf16[8,4096]{1,0:T(8,128)(2,1)S(1)}, bf16[8,720]{1,0:T(8,128)(2,1)S(1)}) custom-call(s32[1]{0:T(128)S(6)} %copy.11.length_hbm, s32[32]{0:T(128)} %parents_hbm.1, s32[8]{0:T(128)} %path_hbm.1, bf16[8,4096]{1,0:T(8,128)(2,1)} %q_ref.1, bf16[8,512]{1,0:T(8,128)(2,1)} %k_ref.1, bf16[8,512]{1,0:T(8,128)(2,1)} %v_ref.1, bf16[512,512]{1,0:T(8,128)(2,1)} %kc_ref.1, ...), custom_call_target="tpu_custom_call" | custom-call | tf_op jit(solution)/shard_map/verify_tree/pallas_call | solution.py:307
  18.6 0.7 %write_out.1 = (bf16[8,4096]{1,0:T(8,128)(2,1)}, bf16[8,720]{1,0:T(8,128)(2,1)}) custom-call(bf16[8,4096]{1,0:T(8,128)(2,1)S(1)} %get-tuple-element.4.att_ref, bf16[8,720]{1,0:T(8,128)(2,1)S(1)} %get-tuple-element.5.out_ref), custom_call_target="tpu_custom_call" | custom-call | tf_op jit(solution)/shard_map/write_out/pallas_call | solution.py:339
where the time goes:
time: 19.4 us; the launch traced here: 19.2 us
  Pallas kernels  17.9 us (92%)
  between operations  1.29 us (7%)
    pallas_call x1, Pallas kernels, local(): pl.pallas_call(functools.partial(kernel, n, own, parents.shape[0]), out_s...  17.3 us
    pallas_call x1, Pallas kernels, local(): pl.pallas_call(write_out, out_shape=shapes, in_specs=(vmem, vmem), out_sp...  0.65 us

commit v1 on v0

v1 whole, which is shorter than its diff:
```python
import functools
import math

import jax
import jax.numpy as jnp
from jax import lax
from jax.experimental import pallas as pl
from jax.experimental.pallas import tpu as pltpu
from jax.sharding import PartitionSpec as P

QUERY_HEADS = 64
KEY_VALUE_HEADS = 8
HEAD_WIDTH = 64
GROUP = QUERY_HEADS // KEY_VALUE_HEADS
LANES = 128
HALF = LANES // 2
SPAN = GROUP * HEAD_WIDTH
PAIRS = SPAN // LANES
CHUNKS = KEY_VALUE_HEADS // 2
CHUNK = 2 * SPAN
ROWS = LANES // (2 * GROUP)
DEPTH = HEAD_WIDTH + 8
TILE = 16
UNIT = 256
LAG = 1
EXCLUDED = -1e30
FLOOR = -1e20
SCALE = HEAD_WIDTH ** (-0.5)
EXPONENT = SCALE * math.log2(math.e)
NT = (((1,), (1,)), ((), ()))
MESH = pl.DeviceIdType.MESH


def partner(me, k, n):
    if n & (n - 1):
        return lax.rem(me + k, n)
    other = me
    bit = 1
    while bit < n:
        if k & bit:
            other = other + bit - 2 * bit * ((me // bit) % 2)
        bit *= 2
    return other


def split(value):
    first = value.astype(jnp.bfloat16).astype(jnp.float32)
    rest = value - first
    second = rest.astype(jnp.bfloat16).astype(jnp.float32)
    return [first, second, rest - second]


def fold(top, total):
    row = lax.broadcasted_iota(jnp.int32, total.shape, 0)
    stat = jnp.zeros_like(total)
    for at, term in enumerate(split(jnp.broadcast_to(top, total.shape)) + split(total)):
        stat = jnp.where(row == at, term, stat)
    return stat


def merge(parts):
    stats = [part[HEAD_WIDTH:] for part in parts]
    tops = [stat[0:1] + stat[1:2] + stat[2:3] for stat in stats]
    totals = [stat[3:4] + stat[4:5] + stat[5:6] for stat in stats]
    top = functools.reduce(jnp.maximum, tops)
    shares = [jnp.exp2((each - top) * EXPONENT) for each in tops]
    total = functools.reduce(jnp.add, [share * each for share, each in zip(shares, totals)])
    merged = functools.reduce(
        jnp.add, [part[:HEAD_WIDTH] * (share / total) for share, part in zip(shares, parts)]
    )
    turned = jnp.concatenate([merged, pltpu.roll(merged, LANES - ROWS, 1)], axis=0).T
    return jnp.concatenate(
        [turned[2 * ROWS * pair : 2 * ROWS * pair + ROWS] for pair in range(2 * PAIRS)], axis=1
    ).astype(jnp.bfloat16)


def kernel(
    n, own, nodes,
    length_hbm, parents_hbm, path_hbm, q_ref, k_ref, v_ref, kc_ref, vc_ref, w_ref,
    att_ref, out_ref,
    length_ref, parents_ref, path_ref, kown, vown,
    qbuf, kbuf, vbuf, wbuf, keys, values, sbuf, rbuf, psend, pbuf, picks, acc,
    load_sem, q_recv, r_recv, p_recv, sends,
):
    me = lax.axis_index("blk")
    rows = q_ref.shape[0]
    wide = n * rows
    cached = kc_ref.shape[0]
    picked = path_hbm.shape[0]
    peers = [partner(me, k, n) for k in range(n - 1, 0, -1)]

    load_q = pltpu.make_async_copy(q_ref, qbuf.at[me], load_sem.at[0])
    load_q.start()
    small_loads = [
        pltpu.make_async_copy(src, dst, load_sem.at[4 + i])
        for i, (src, dst) in enumerate((
            (parents_hbm, parents_ref), (length_hbm, length_ref), (path_hbm, path_ref),
            (k_ref, kown), (v_ref, vown),
        ))
    ]
    for copy in small_loads:
        copy.start()
    load_k = pltpu.make_async_copy(kc_ref, kbuf, load_sem.at[1])
    load_v = pltpu.make_async_copy(vc_ref, vbuf, load_sem.at[2])
    load_w = pltpu.make_async_copy(w_ref, wbuf, load_sem.at[3])
    load_k.start()
    load_v.start()

    barrier = pltpu.get_barrier_semaphore()
    for peer in peers:
        pl.semaphore_signal(barrier, inc=1, device_id={"blk": peer}, device_id_type=MESH)
    pl.semaphore_wait(barrier, n - 1)

    def q_copy(c, peer):
        columns = pl.ds(c * CHUNK, CHUNK)
        return pltpu.make_async_remote_copy(
            src_ref=qbuf.at[me, :, columns], dst_ref=qbuf.at[me, :, columns],
            send_sem=sends.at[0], recv_sem=q_recv.at[c],
            device_id={"blk": peer}, device_id_type=MESH,
        )

    def r_copy(c, peer):
        return pltpu.make_async_remote_copy(
            src_ref=sbuf.at[c, peer], dst_ref=rbuf.at[c, me],
            send_sem=sends.at[1], recv_sem=r_recv.at[c],
            device_id={"blk": peer}, device_id_type=MESH,
        )

    def p_copy(c, peer):
        return pltpu.make_async_remote_copy(
            src_ref=psend.at[c], dst_ref=pbuf.at[c, me],
            send_sem=sends.at[2], recv_sem=p_recv.at[c],
            device_id={"blk": peer}, device_id_type=MESH,
        )

    def arrived(block, sem):
        pltpu.make_async_copy(block, block, sem).wait()

    others = pl.ds(0, n - 1)
    load_q.wait()
    for c in range(CHUNKS):
        for peer in peers:
            q_copy(c, peer).start()
    load_w.start()

    for copy in small_loads:
        copy.wait()

    up = lax.broadcasted_iota(jnp.int32, (wide, wide), 0)
    down = lax.broadcasted_iota(jnp.int32, (wide, wide), 1)
    up_node = up // rows * own + up % rows
    links = jnp.where(up == down, 1.0, 0.0)
    for i in range(1, nodes):
        at = i // own * rows + i % own
        links = jnp.where((down == at) & (up_node == parents_ref[i]) & (up % rows < own), 1.0, links)
    for squaring in range(max(1, math.ceil(math.log2(nodes)))):
        half = links.astype(jnp.bfloat16)
        links = jnp.minimum(jnp.dot(half, half, preferred_element_type=jnp.float32), 1.0)
    source = lax.broadcasted_iota(jnp.int32, (wide, LANES), 0)
    lane = lax.broadcasted_iota(jnp.int32, (wide, LANES), 1)
    spare = lane % HALF
    mine = jnp.where((source == me * rows + spare - 1) & (spare >= 1) & (spare <= own), 1.0, 0.0)
    related = lax.dot_general(
        links.astype(jnp.bfloat16), mine.astype(jnp.bfloat16), (((0,), (0,)), ((), ())),
        preferred_element_type=jnp.float32,
    )
    marks = jnp.where(
        spare == 0, 1.0,
        jnp.where((spare <= own) & (related < 0.5), EXCLUDED, 0.0),
    )

    size = n * HALF
    at = lax.broadcasted_iota(jnp.int32, (2 * size, LANES), 0)
    goal = lax.broadcasted_iota(jnp.int32, (2 * size, LANES), 1)
    spot_node = at % size // HALF * own + at % ROWS
    wanted = jnp.full((2 * size, LANES), -1, jnp.int32)
    for k in range(picked):
        wanted = jnp.where(goal % ROWS == k, path_ref[k], wanted)
    same = (at // size == goal // HALF) & (at % HALF // ROWS == goal % HALF // ROWS)
    picks[...] = jnp.where(
        same & (wanted == spot_node) & (at % ROWS < own), 1.0, 0.0
    ).astype(jnp.bfloat16)

    place = lax.broadcasted_iota(jnp.int32, (cached, LANES), 0) + me * cached
    column = lax.broadcasted_iota(jnp.int32, (cached, LANES), 1)
    spent = jnp.where((column % HALF == 0) & (place >= length_ref[0]), EXCLUDED, 0.0)
    node = lax.broadcasted_iota(jnp.int32, (TILE, LANES), 0)
    node_lane = lax.broadcasted_iota(jnp.int32, (TILE, LANES), 1)
    node_spare = node_lane % HALF
    tags = jnp.where(
        node < own, jnp.where(node_spare == node + 1, 1.0, 0.0),
        jnp.where(node_spare == 0, EXCLUDED, 0.0),
    )
    blank = jnp.zeros((LANES - rows, LANES), jnp.float32)
    load_k.wait()
    for h in range(KEY_VALUE_HEADS):
        columns = slice(h // 2 * LANES, (h // 2 + 1) * LANES)
        held = (column < HALF) if h % 2 == 0 else (column >= HALF)
        node_held = (node_lane < HALF) if h % 2 == 0 else (node_lane >= HALF)
        keys[h, pl.ds(0, cached)] = jnp.where(
            held, kbuf[:, columns].astype(jnp.float32), spent
        ).astype(jnp.bfloat16)
        fresh = jnp.concatenate([kown[:, columns].astype(jnp.float32), blank], axis=0)
        keys[h, pl.ds(cached, TILE)] = jnp.where(node_held, fresh[:TILE], tags).astype(jnp.bfloat16)
    load_v.wait()
    for c in range(CHUNKS):
        columns = slice(c * LANES, (c + 1) * LANES)
        fresh = jnp.concatenate([vown[:, columns].astype(jnp.float32), blank], axis=0)
        turned = vbuf[:, columns].astype(jnp.float32).T.astype(jnp.bfloat16)
        fresh = fresh.T.astype(jnp.bfloat16)
        for side in range(2):
            half = slice(side * HALF, (side + 1) * HALF)
            values[2 * c + side, pl.ds(0, HALF), pl.ds(0, cached)] = turned[half]
            values[2 * c + side, pl.ds(0, HALF), pl.ds(cached, LANES)] = fresh[half]
            values[2 * c + side, pl.ds(HALF, 16)] = jnp.ones((16, cached + LANES), jnp.bfloat16)

    low = lax.broadcasted_iota(jnp.int32, (rows, LANES), 1) < HALF
    deep_low = lax.broadcasted_iota(jnp.int32, (DEPTH, LANES), 1) < HALF
    for c in range(CHUNKS):
        arrived(qbuf.at[others, :, pl.ds(c * CHUNK, CHUNK)], q_recv.at[c])
        q = qbuf[:, :, c * CHUNK : (c + 1) * CHUNK].astype(jnp.float32)
        asked = []
        for side in range(2):
            keep = low if side == 0 else jnp.logical_not(low)
            stacked = []
            for d in range(n):
                extra = marks[d * rows : (d + 1) * rows]
                for pair in range(PAIRS):
                    start = side * SPAN + pair * LANES
                    tile = q[d, :, start : start + LANES]
                    turned = pltpu.roll(tile, HALF, 1)
                    even, odd = (tile, turned) if side == 0 else (turned, tile)
                    stacked.append(jnp.where(keep, even, extra))
                    stacked.append(jnp.where(keep, odd, extra))
            queries = jnp.concatenate(stacked, axis=0).astype(jnp.bfloat16)
            asked += [
                (2 * c + side, queries[start : start + UNIT]) for start in range(0, size, UNIT)
            ]

        def score(h, queries):
            return lax.dot_general(keys[h], queries, NT, preferred_element_type=jnp.float32)

        def weigh(h, scores):
            top = jnp.maximum(jnp.max(scores, axis=0, keepdims=True), FLOOR)
            weights = jnp.exp2((scores - top) * EXPONENT).astype(jnp.bfloat16)
            weighted = jnp.dot(
                values[h, :, pl.ds(0, cached)], weights[:cached], preferred_element_type=jnp.float32
            ) + jnp.dot(
                values[h, :, pl.ds(cached, TILE)], weights[cached:],
                preferred_element_type=jnp.float32,
            )
            return jnp.concatenate([weighted[:HALF], fold(top, weighted[HALF:DEPTH])], axis=0)

        done, waiting = [], []
        for h, queries in asked:
            waiting.append((h, score(h, queries)))
            if len(waiting) > LAG:
                done.append(weigh(*waiting.pop(0)))
        done += [weigh(*each) for each in waiting]
        per = len(done) // 2
        full = [jnp.concatenate(done[side * per : (side + 1) * per], axis=1) for side in range(2)]
        for d in range(n):
            block = slice(d // 2 * LANES, (d // 2 + 1) * LANES)
            left, right = full[0][:, block], full[1][:, block]
            if d % 2 == 0:
                right = pltpu.roll(right, HALF, 1)
            else:
                left = pltpu.roll(left, HALF, 1)
            sbuf[c, d] = jnp.where(deep_low, left, right).astype(jnp.bfloat16)
        for peer in peers:
            r_copy(c, peer).start()
        psend[c] = jnp.dot(
            jnp.concatenate(full, axis=1).astype(jnp.bfloat16), picks[...],
            preferred_element_type=jnp.float32,
        ).astype(jnp.bfloat16)
        for peer in peers:
            p_copy(c, peer).start()

    load_w.wait()
    acc[...] = jnp.zeros_like(acc)
    for c in range(CHUNKS):
        columns = pl.ds(c * CHUNK, CHUNK)
        arrived(rbuf.at[c, others], r_recv.at[c])
        arrived(pbuf.at[c, others], p_recv.at[c])
        parts = [sbuf[c, me]] + [rbuf[c, peer] for peer in peers]
        att_ref[:, columns] = merge([part.astype(jnp.float32) for part in parts])
        parts = [psend[c]] + [pbuf[c, peer] for peer in peers]
        acc[...] += lax.dot_general(
            merge([part.astype(jnp.float32) for part in parts]), wbuf[:, columns], NT,
            preferred_element_type=jnp.float32,
        )
    out_ref[...] = acc[...].astype(jnp.bfloat16)

    arrived(qbuf.at[others], sends.at[0])
    arrived(rbuf.at[:, others], sends.at[1])
    arrived(pbuf.at[:, others], sends.at[2])


def write_out(att_ref, out_ref, att_hbm, out_hbm, sems):
    copies = [
        pltpu.make_async_copy(att_ref, att_hbm, sems.at[0]),
        pltpu.make_async_copy(out_ref, out_hbm, sems.at[1]),
    ]
    for copy in copies:
        copy.start()
    for copy in copies:
        copy.wait()


def local(
    n,
    draft_node_queries,
    draft_node_keys,
    draft_node_values,
    paged_key_cache,
    paged_value_cache,
    context_length,
    parents,
    accepted_path,
    out_weight,
):
    own = draft_node_queries.shape[0]
    rows = -(-own // 8) * 8
    if rows != own:
        pad = ((0, rows - own), (0, 0))
        draft_node_queries = jnp.pad(draft_node_queries, pad)
        draft_node_keys = jnp.pad(draft_node_keys, pad)
        draft_node_values = jnp.pad(draft_node_values, pad)
    cached, cache_width = paged_key_cache.shape
    picked = accepted_path.shape[0]
    q_width = QUERY_HEADS * HEAD_WIDTH
    vmem = pl.BlockSpec(memory_space=pltpu.VMEM)
    anywhere = pl.BlockSpec(memory_space=pltpu.HBM)
    shapes = (
        jax.ShapeDtypeStruct((rows, q_width), jnp.bfloat16),
        jax.ShapeDtypeStruct((picked, out_weight.shape[0]), jnp.bfloat16),
    )
    held = pl.pallas_call(
        functools.partial(kernel, n, own, parents.shape[0]),
        out_shape=tuple(pltpu.VMEM(shape.shape, shape.dtype) for shape in shapes),
        in_specs=[anywhere] * 9,
        out_specs=(vmem, vmem),
        scratch_shapes=[
            pltpu.SMEM(context_length.shape, jnp.int32),
            pltpu.SMEM(parents.shape, jnp.int32),
            pltpu.SMEM(accepted_path.shape, jnp.int32),
            pltpu.VMEM((rows, cache_width), jnp.bfloat16),
            pltpu.VMEM((rows, cache_width), jnp.bfloat16),
            pltpu.VMEM((n, rows, q_width), jnp.bfloat16),
            pltpu.VMEM((cached, cache_width), jnp.bfloat16),
            pltpu.VMEM((cached, cache_width), jnp.bfloat16),
            pltpu.VMEM(out_weight.shape, jnp.bfloat16),
            pltpu.VMEM((KEY_VALUE_HEADS, cached + TILE, LANES), jnp.bfloat16),
            pltpu.VMEM((KEY_VALUE_HEADS, HALF + 16, cached + LANES), jnp.bfloat16),
            pltpu.VMEM((CHUNKS, n, DEPTH, LANES), jnp.bfloat16),
            pltpu.VMEM((CHUNKS, n, DEPTH, LANES), jnp.bfloat16),
            pltpu.VMEM((CHUNKS, DEPTH, LANES), jnp.bfloat16),
            pltpu.VMEM((CHUNKS, n, DEPTH, LANES), jnp.bfloat16),
            pltpu.VMEM((2 * n * HALF, LANES), jnp.bfloat16),
            pltpu.VMEM((picked, out_weight.shape[0]), jnp.float32),
            pltpu.SemaphoreType.DMA((9,)),
            pltpu.SemaphoreType.DMA((CHUNKS,)),
            pltpu.SemaphoreType.DMA((CHUNKS,)),
            pltpu.SemaphoreType.DMA((CHUNKS,)),
            pltpu.SemaphoreType.DMA((3,)),
        ],
        compiler_params=pltpu.CompilerParams(
            collective_id=0, has_side_effects=True, vmem_limit_bytes=56 * 1024 * 1024
        ),
        name="verify_tree",
    )(
        context_length, parents, accepted_path,
        draft_node_queries, draft_node_keys, draft_node_values,
        paged_key_cache, paged_value_cache, out_weight,
    )
    attention, path_output = pl.pallas_call(
        write_out,
        out_shape=shapes,
        in_specs=(vmem, vmem),
        out_specs=(anywhere, anywhere),
        scratch_shapes=[pltpu.SemaphoreType.DMA((2,))],
        compiler_params=pltpu.CompilerParams(vmem_limit_bytes=1024 * 1024),
        name="write_out",
    )(*held)
    return attention[:own], path_output


def solution(mesh):
    in_specs = (
        P(("req", "blk"), None),
        P(("req", "blk"), None),
        P(("req", "blk"), None),
        P(("req", "blk"), None),
        P(("req", "blk"), None),
        P("req"),
        P("req"),
        P("req"),
        P("blk", None),
    )
    out_specs = (P(("req", "blk"), None), P("req", "blk"))
    return jax.shard_map(
        functools.partial(local, mesh.shape["blk"]),
        mesh=mesh, in_specs=in_specs, out_specs=out_specs, check_vma=False,
    )
```

time: 19.4 us -> 18.5 us (0.954)
  Pallas kernels: 17.9 us -> 17 us
    pallas_call x1, Pallas kernels: 17.3 us -> 16.4 us  [local(): pl.pallas_call(functools.partial(kernel, n, own, parents.shape[0]), out_s...]
where the time goes in v1:
time: 18.5 us; the launch traced here: 18.3 us
  Pallas kernels  17 us (92%)
  between operations  1.29 us (7%)
    pallas_call x1, Pallas kernels, local(): pl.pallas_call(functools.partial(kernel, n, own, parents.shape[0]), out_s...  16.4 us
    pallas_call x1, Pallas kernels, local(): pl.pallas_call(write_out, out_shape=shapes, in_specs=(vmem, vmem), out_sp...  0.65 us

profile of v1, /device:TPU:0, one launch (start us, length us, event | category | flops | bytes accessed | tf_op | source)
XLA Modules:
  0.0 18.3 jit_solution(14560689633625494106)
XLA Ops:
  1.3 16.4 %verify_tree.1 = (bf16[8,4096]{1,0:T(8,128)(2,1)S(1)}, bf16[8,720]{1,0:T(8,128)(2,1)S(1)}) custom-call(s32[1]{0:T(128)S(6)} %copy.11.length_hbm, s32[32]{0:T(128)} %parents_hbm.1, s32[8]{0:T(128)} %path_hbm.1, bf16[8,4096]{1,0:T(8,128)(2,1)} %q_ref.1, bf16[8,512]{1,0:T(8,128)(2,1)} %k_ref.1, bf16[8,512]{1,0:T(8,128)(2,1)} %v_ref.1, bf16[512,512]{1,0:T(8,128)(2,1)} %kc_ref.1, ...), custom_call_target="tpu_custom_call" | custom-call | tf_op jit(solution)/shard_map/verify_tree/pallas_call | solution.py:338
  17.7 0.7 %write_out.1 = (bf16[8,4096]{1,0:T(8,128)(2,1)}, bf16[8,720]{1,0:T(8,128)(2,1)}) custom-call(bf16[8,4096]{1,0:T(8,128)(2,1)S(1)} %get-tuple-element.4.att_ref, bf16[8,720]{1,0:T(8,128)(2,1)S(1)} %get-tuple-element.5.out_ref), custom_call_target="tpu_custom_call" | custom-call | tf_op jit(solution)/shard_map/write_out/pallas_call | solution.py:376

commit v2 on v1

--- a/solution.py
+++ b/solution.py
@@ -259,6 +259,12 @@
         done += [weigh(*each) for each in waiting]
         per = len(done) // 2
         full = [jnp.concatenate(done[side * per : (side + 1) * per], axis=1) for side in range(2)]
+        psend[c] = jnp.dot(
+            jnp.concatenate(full, axis=1).astype(jnp.bfloat16), picks[...],
+            preferred_element_type=jnp.float32,
+        ).astype(jnp.bfloat16)
+        for peer in peers:
+            p_copy(c, peer).start()
         for d in range(n):
             block = slice(d // 2 * LANES, (d // 2 + 1) * LANES)
             left, right = full[0][:, block], full[1][:, block]
@@ -269,27 +275,22 @@
             sbuf[c, d] = jnp.where(deep_low, left, right).astype(jnp.bfloat16)
         for peer in peers:
             r_copy(c, peer).start()
-        psend[c] = jnp.dot(
-            jnp.concatenate(full, axis=1).astype(jnp.bfloat16), picks[...],
-            preferred_element_type=jnp.float32,
-        ).astype(jnp.bfloat16)
-        for peer in peers:
-            p_copy(c, peer).start()
 
     load_w.wait()
     acc[...] = jnp.zeros_like(acc)
     for c in range(CHUNKS):
         columns = pl.ds(c * CHUNK, CHUNK)
-        arrived(rbuf.at[c, others], r_recv.at[c])
         arrived(pbuf.at[c, others], p_recv.at[c])
-        parts = [sbuf[c, me]] + [rbuf[c, peer] for peer in peers]
-        att_ref[:, columns] = merge([part.astype(jnp.float32) for part in parts])
         parts = [psend[c]] + [pbuf[c, peer] for peer in peers]
         acc[...] += lax.dot_general(
             merge([part.astype(jnp.float32) for part in parts]), wbuf[:, columns], NT,
             preferred_element_type=jnp.float32,
         )
-    out_ref[...] = acc[...].astype(jnp.bfloat16)
+        if c == CHUNKS - 1:
+            out_ref[...] = acc[...].astype(jnp.bfloat16)
+        arrived(rbuf.at[c, others], r_recv.at[c])
+        parts = [sbuf[c, me]] + [rbuf[c, peer] for peer in peers]
+        att_ref[:, columns] = merge([part.astype(jnp.float32) for part in parts])
 
     arrived(qbuf.at[others], sends.at[0])
     arrived(rbuf.at[:, others], sends.at[1])

time: 18.5 us -> 18.1 us (0.978)
  Pallas kernels: 17 us -> 16.7 us
    pallas_call x1, Pallas kernels: 16.4 us -> 16 us  [local(): pl.pallas_call(functools.partial(kernel, n, own, parents.shape[0]), out_s...]
where the time goes in v2:
time: 18.1 us; the launch traced here: 18 us
  Pallas kernels  16.7 us (92%)
  between operations  1.29 us (7%)
    pallas_call x1, Pallas kernels, local(): pl.pallas_call(functools.partial(kernel, n, own, parents.shape[0]), out_s...  16 us
    pallas_call x1, Pallas kernels, local(): pl.pallas_call(write_out, out_shape=shapes, in_specs=(vmem, vmem), out_sp...  0.65 us

profile of v2, /device:TPU:0, one launch (start us, length us, event | category | flops | bytes accessed | tf_op | source)
XLA Modules:
  0.0 18.0 jit_solution(1831101926740924578)
XLA Ops:
  1.3 16.0 %verify_tree.1 = (bf16[8,4096]{1,0:T(8,128)(2,1)S(1)}, bf16[8,720]{1,0:T(8,128)(2,1)S(1)}) custom-call(s32[1]{0:T(128)S(6)} %copy.11.length_hbm, s32[32]{0:T(128)} %parents_hbm.1, s32[8]{0:T(128)} %path_hbm.1, bf16[8,4096]{1,0:T(8,128)(2,1)} %q_ref.1, bf16[8,512]{1,0:T(8,128)(2,1)} %k_ref.1, bf16[8,512]{1,0:T(8,128)(2,1)} %v_ref.1, bf16[512,512]{1,0:T(8,128)(2,1)} %kc_ref.1, ...), custom_call_target="tpu_custom_call" | custom-call | tf_op jit(solution)/shard_map/verify_tree/pallas_call | solution.py:339
  17.3 0.7 %write_out.1 = (bf16[8,4096]{1,0:T(8,128)(2,1)}, bf16[8,720]{1,0:T(8,128)(2,1)}) custom-call(bf16[8,4096]{1,0:T(8,128)(2,1)S(1)} %get-tuple-element.4.att_ref, bf16[8,720]{1,0:T(8,128)(2,1)S(1)} %get-tuple-element.5.out_ref), custom_call_target="tpu_custom_call" | custom-call | tf_op jit(solution)/shard_map/write_out/pallas_call | solution.py:377

commit v3 on v2

--- a/solution.py
+++ b/solution.py
@@ -21,8 +21,6 @@
 ROWS = LANES // (2 * GROUP)
 DEPTH = HEAD_WIDTH + 8
 TILE = 16
-UNIT = 256
-LAG = 1
 EXCLUDED = -1e30
 FLOOR = -1e20
 SCALE = HEAD_WIDTH ** (-0.5)
@@ -91,6 +89,9 @@
 
     load_q = pltpu.make_async_copy(q_ref, qbuf.at[me], load_sem.at[0])
     load_q.start()
+    barrier = pltpu.get_barrier_semaphore()
+    for peer in peers:
+        pl.semaphore_signal(barrier, inc=1, device_id={"blk": peer}, device_id_type=MESH)
     small_loads = [
         pltpu.make_async_copy(src, dst, load_sem.at[4 + i])
         for i, (src, dst) in enumerate((
@@ -106,9 +107,6 @@
     load_k.start()
     load_v.start()
 
-    barrier = pltpu.get_barrier_semaphore()
-    for peer in peers:
-        pl.semaphore_signal(barrier, inc=1, device_id={"blk": peer}, device_id_type=MESH)
     pl.semaphore_wait(barrier, n - 1)
 
     def q_copy(c, peer):
@@ -216,49 +214,51 @@
 
     low = lax.broadcasted_iota(jnp.int32, (rows, LANES), 1) < HALF
     deep_low = lax.broadcasted_iota(jnp.int32, (DEPTH, LANES), 1) < HALF
+    def ask(h):
+        side = h % 2
+        columns = pl.ds(h * SPAN, SPAN)
+        q = qbuf[:, :, columns].astype(jnp.float32)
+        keep = low if side == 0 else jnp.logical_not(low)
+        stacked = []
+        for d in range(n):
+            extra = marks[d * rows : (d + 1) * rows]
+            for pair in range(PAIRS):
+                start = pair * LANES
+                tile = q[d, :, start : start + LANES]
+                turned = pltpu.roll(tile, HALF, 1)
+                even, odd = (tile, turned) if side == 0 else (turned, tile)
+                stacked.append(jnp.where(keep, even, extra))
+                stacked.append(jnp.where(keep, odd, extra))
+        queries = jnp.concatenate(stacked, axis=0).astype(jnp.bfloat16)
+        return lax.dot_general(keys[h], queries, NT, preferred_element_type=jnp.float32)
+
+    def weigh(h, scores):
+        top = jnp.maximum(jnp.max(scores, axis=0, keepdims=True), FLOOR)
+        weights = jnp.exp2((scores - top) * EXPONENT).astype(jnp.bfloat16)
+        weighted = jnp.dot(
+            values[h, :, pl.ds(0, cached)], weights[:cached], preferred_element_type=jnp.float32
+        ) + jnp.dot(
+            values[h, :, pl.ds(cached, TILE)], weights[cached:],
+            preferred_element_type=jnp.float32,
+        )
+        return jnp.concatenate([weighted[:HALF], fold(top, weighted[HALF:DEPTH])], axis=0)
+
+    def reach(c):
+        arrived(qbuf.at[others, :, pl.ds(c * CHUNK, CHUNK)], q_recv.at[c])
+
+    ahead = []
     for c in range(CHUNKS):
-        arrived(qbuf.at[others, :, pl.ds(c * CHUNK, CHUNK)], q_recv.at[c])
-        q = qbuf[:, :, c * CHUNK : (c + 1) * CHUNK].astype(jnp.float32)
-        asked = []
+        if not ahead:
+            reach(c)
+            ahead = [ask(2 * c), ask(2 * c + 1)]
+        full, scores, ahead = [], ahead, []
+        early = 0 <= c < CHUNKS - 1
+        if early:
+            reach(c + 1)
         for side in range(2):
-            keep = low if side == 0 else jnp.logical_not(low)
-            stacked = []
-            for d in range(n):
-                extra = marks[d * rows : (d + 1) * rows]
-                for pair in range(PAIRS):
-                    start = side * SPAN + pair * LANES
-                    tile = q[d, :, start : start + LANES]
-                    turned = pltpu.roll(tile, HALF, 1)
-                    even, odd = (tile, turned) if side == 0 else (turned, tile)
-                    stacked.append(jnp.where(keep, even, extra))
-                    stacked.append(jnp.where(keep, odd, extra))
-            queries = jnp.concatenate(stacked, axis=0).astype(jnp.bfloat16)
-            asked += [
-                (2 * c + side, queries[start : start + UNIT]) for start in range(0, size, UNIT)
-            ]
-
-        def score(h, queries):
-            return lax.dot_general(keys[h], queries, NT, preferred_element_type=jnp.float32)
-
-        def weigh(h, scores):
-            top = jnp.maximum(jnp.max(scores, axis=0, keepdims=True), FLOOR)
-            weights = jnp.exp2((scores - top) * EXPONENT).astype(jnp.bfloat16)
-            weighted = jnp.dot(
-                values[h, :, pl.ds(0, cached)], weights[:cached], preferred_element_type=jnp.float32
-            ) + jnp.dot(
-                values[h, :, pl.ds(cached, TILE)], weights[cached:],
-                preferred_element_type=jnp.float32,
-            )
-            return jnp.concatenate([weighted[:HALF], fold(top, weighted[HALF:DEPTH])], axis=0)
-
-        done, waiting = [], []
-        for h, queries in asked:
-            waiting.append((h, score(h, queries)))
-            if len(waiting) > LAG:
-                done.append(weigh(*waiting.pop(0)))
-        done += [weigh(*each) for each in waiting]
-        per = len(done) // 2
-        full = [jnp.concatenate(done[side * per : (side + 1) * per], axis=1) for side in range(2)]
+            if early:
+                ahead.append(ask(2 * c + 2 + side))
+            full.append(weigh(2 * c + side, scores[side]))
         psend[c] = jnp.dot(
             jnp.concatenate(full, axis=1).astype(jnp.bfloat16), picks[...],
             preferred_element_type=jnp.float32,

time: 18.1 us -> 18 us (level)
  no operation moved by 1% of the time
where the time goes in v3:
time: 18 us; the launch traced here: 17.9 us
  Pallas kernels  16.6 us (92%)
  between operations  1.29 us (7%)
    pallas_call x1, Pallas kernels, local(): pl.pallas_call(functools.partial(kernel, n, own, parents.shape[0]), out_s...  15.9 us
    pallas_call x1, Pallas kernels, local(): pl.pallas_call(write_out, out_shape=shapes, in_specs=(vmem, vmem), out_sp...  0.65 us

profile of v3, /device:TPU:0, one launch (start us, length us, event | category | flops | bytes accessed | tf_op | source)
XLA Modules:
  0.0 17.9 jit_solution(8147154754430502717)
XLA Ops:
  1.3 15.9 %verify_tree.1 = (bf16[8,4096]{1,0:T(8,128)(2,1)S(1)}, bf16[8,720]{1,0:T(8,128)(2,1)S(1)}) custom-call(s32[1]{0:T(128)S(6)} %copy.11.length_hbm, s32[32]{0:T(128)} %parents_hbm.1, s32[8]{0:T(128)} %path_hbm.1, bf16[8,4096]{1,0:T(8,128)(2,1)} %q_ref.1, bf16[8,512]{1,0:T(8,128)(2,1)} %k_ref.1, bf16[8,512]{1,0:T(8,128)(2,1)} %v_ref.1, bf16[512,512]{1,0:T(8,128)(2,1)} %kc_ref.1, ...), custom_call_target="tpu_custom_call" | custom-call | tf_op jit(solution)/shard_map/verify_tree/pallas_call | solution.py:339
  17.2 0.7 %write_out.1 = (bf16[8,4096]{1,0:T(8,128)(2,1)}, bf16[8,720]{1,0:T(8,128)(2,1)}) custom-call(bf16[8,4096]{1,0:T(8,128)(2,1)S(1)} %get-tuple-element.4.att_ref, bf16[8,720]{1,0:T(8,128)(2,1)S(1)} %get-tuple-element.5.out_ref), custom_call_target="tpu_custom_call" | custom-call | tf_op jit(solution)/shard_map/write_out/pallas_call | solution.py:377

commit v4 on v3

--- a/solution.py
+++ b/solution.py
@@ -106,6 +106,7 @@
     load_w = pltpu.make_async_copy(w_ref, wbuf, load_sem.at[3])
     load_k.start()
     load_v.start()
+    load_w.start()
 
     pl.semaphore_wait(barrier, n - 1)
 
@@ -139,7 +140,6 @@
     for c in range(CHUNKS):
         for peer in peers:
             q_copy(c, peer).start()
-    load_w.start()
 
     for copy in small_loads:
         copy.wait()

time: 18 us -> 18 us (level)
  no operation moved by 1% of the time
where the time goes in v4:
time: 18 us; the launch traced here: 17.9 us
  Pallas kernels  16.6 us (92%)
  between operations  1.29 us (7%)
    pallas_call x1, Pallas kernels, local(): pl.pallas_call(functools.partial(kernel, n, own, parents.shape[0]), out_s...  15.9 us
    pallas_call x1, Pallas kernels, local(): pl.pallas_call(write_out, out_shape=shapes, in_specs=(vmem, vmem), out_sp...  0.65 us

profile of v4, /device:TPU:0, one launch (start us, length us, event | category | flops | bytes accessed | tf_op | source)
XLA Modules:
  0.0 17.9 jit_solution(14726602757824700098)
XLA Ops:
  1.3 15.9 %verify_tree.1 = (bf16[8,4096]{1,0:T(8,128)(2,1)S(1)}, bf16[8,720]{1,0:T(8,128)(2,1)S(1)}) custom-call(s32[1]{0:T(128)S(6)} %copy.11.length_hbm, s32[32]{0:T(128)} %parents_hbm.1, s32[8]{0:T(128)} %path_hbm.1, bf16[8,4096]{1,0:T(8,128)(2,1)} %q_ref.1, bf16[8,512]{1,0:T(8,128)(2,1)} %k_ref.1, bf16[8,512]{1,0:T(8,128)(2,1)} %v_ref.1, bf16[512,512]{1,0:T(8,128)(2,1)} %kc_ref.1, ...), custom_call_target="tpu_custom_call" | custom-call | tf_op jit(solution)/shard_map/verify_tree/pallas_call | solution.py:339
  17.2 0.7 %write_out.1 = (bf16[8,4096]{1,0:T(8,128)(2,1)}, bf16[8,720]{1,0:T(8,128)(2,1)}) custom-call(bf16[8,4096]{1,0:T(8,128)(2,1)S(1)} %get-tuple-element.4.att_ref, bf16[8,720]{1,0:T(8,128)(2,1)S(1)} %get-tuple-element.5.out_ref), custom_call_target="tpu_custom_call" | custom-call | tf_op jit(solution)/shard_map/write_out/pallas_call | solution.py:377
